TPU v7x, 8 devices: a whole 2x2x1 slice. The times are simulated.
8 devices in a mesh: col: 2 (over z, y), row: 2 (over x), depth: 2 (over core).
Axes of the slice: x: 2, y: 2, z: 1, core: 2. Of those that a mesh axis runs over, the one named last changes fastest.
Arguments:
- a_mat: bfloat16 [3072, 6144], P(('depth', 'row', 'col'))
- b_mat: bfloat16 [6144, 5120], P(('depth', 'row', 'col'))
Outputs:
- output: bfloat16 [3072, 5120], P(('depth', 'row', 'col'))
All inputs are finite; a program needn't handle non-finite values.
Results may differ from a plain program's by a relative error of at most 0.001.
Values are sent between devices in bfloat16 or wider.
A program may use at most 1 GiB of HBM per device.

v0:
```python
import jax
import jax.numpy as jnp
from jax import lax
from jax.experimental import pallas as pl
from jax.experimental.pallas import tpu as pltpu
from jax.sharding import PartitionSpec as P

MESH = pl.DeviceIdType.MESH
TN = 512
LAG = 2
AHEAD = 2
ROUND = 16
ROUND_N = 384
EXTRA = 48
EARLY = 304


def kernel(a_ref, b_ref, c_ref, own_ref, nbr_ref, b_buf, a_own, a_nbr, p_own, p_snd, p_rcv, a_fwd,
           ld_a, ld_b, a_snd_sem, a_rcv_sem, b_snd_sem, b_rcv_sem, d_snd_sem, d_rcv_sem,
           r_snd_sem, r_rcv_sem, c_snd_sem, c_rcv_sem, f_snd_sem, f_rcv_sem, fwd_sem,
           pair_sem, core_sem, round_buf, round_snd, round_rcv, early_rcv, early_sem):
    depth, row, col = lax.axis_index("depth"), lax.axis_index("row"), lax.axis_index("col")
    to_x, to_y, to_d = {"row": 1 - row}, {"col": 1 - col}, {"depth": 1 - depth}
    rows, k_rows = a_ref.shape[0], b_ref.shape[0]
    half = rows // 2
    n_chunks, n_here = b_buf.shape[0], p_own.shape[0]

    def k_block(place, r):
        d = 1 - depth if place % 2 else depth
        c = 1 - col if place // 2 else col
        return pl.ds(pl.multiple_of((d * 4 + r * 2 + c) * k_rows, k_rows), k_rows)

    def slot(place):
        return pl.ds(place * k_rows, k_rows)

    def cols(j):
        return pl.ds(pl.multiple_of(j * TN, TN), TN)

    def load_a(place):
        return pltpu.make_async_copy(a_ref.at[:, k_block(place, row)], a_own.at[:, slot(place)], ld_a.at[place])

    def load_b(j):
        return pltpu.make_async_copy(b_ref.at[:, cols(j)], b_buf.at[j, slot(0), :], ld_b.at[j])

    pieces = [(0, half, p) for p in range(4)] + [(half, half, p) for p in range(2)]
    pieces += [(half, half - EXTRA, p) for p in (2, 3)] + [(rows - EXTRA, EXTRA, p) for p in (2, 3)]
    last = len(pieces) - 2

    def send_a(i):
        start, size, place = pieces[i]
        return pltpu.make_async_remote_copy(
            src_ref=a_ref.at[pl.ds(start, size), k_block(place, 1 - row)],
            dst_ref=a_nbr.at[pl.ds(start, size), slot(place)],
            send_sem=a_snd_sem.at[i], recv_sem=a_rcv_sem.at[i], device_id=to_x, device_id_type=MESH)

    def hand_over(i):
        start, size, place = pieces[last + i]
        return pltpu.make_async_remote_copy(
            src_ref=a_ref.at[pl.ds(start, size), k_block(place, 1 - row)], dst_ref=a_fwd.at[i],
            send_sem=f_snd_sem.at[i], recv_sem=f_rcv_sem.at[i], device_id=to_d, device_id_type=MESH)

    def send_for_other(i):
        start, size, place = pieces[last + i]
        return pltpu.make_async_remote_copy(
            src_ref=a_fwd.at[i], dst_ref=a_nbr.at[pl.ds(start, size), slot(place)],
            send_sem=fwd_sem.at[i], recv_sem=a_rcv_sem.at[last + i],
            device_id={"row": 1 - row, "depth": 0}, device_id_type=MESH)

    def send_b(j):
        return pltpu.make_async_remote_copy(
            src_ref=b_ref.at[:, cols(j)], dst_ref=b_buf.at[j, slot(2), :],
            send_sem=b_snd_sem.at[j], recv_sem=b_rcv_sem.at[j], device_id=to_y, device_id_type=MESH)

    def send_d(j):
        return pltpu.make_async_remote_copy(
            src_ref=b_ref.at[:, cols(j)], dst_ref=b_buf.at[j, slot(1), :],
            send_sem=d_snd_sem.at[j], recv_sem=d_rcv_sem.at[j], device_id=to_d, device_id_type=MESH)

    def relay(j):
        return pltpu.make_async_remote_copy(
            src_ref=b_buf.at[j, slot(2), :], dst_ref=b_buf.at[j, slot(3), :],
            send_sem=r_snd_sem.at[j], recv_sem=r_rcv_sem.at[j], device_id=to_d, device_id_type=MESH)

    tail_rows = pl.ds(rows - ROUND, ROUND)
    source = (depth == 1) & (row == 1) & (col == 0)
    first_relay = (depth == 1) & (row == 1) & (col == 1)
    second_relay = (depth == 1) & (row == 0) & (col == 1)

    def send_tail():
        return pltpu.make_async_remote_copy(
            src_ref=p_snd.at[n_here - 1, tail_rows, pl.ds(0, ROUND_N)], dst_ref=p_rcv.at[n_here - 1, tail_rows, pl.ds(0, ROUND_N)],
            send_sem=round_snd.at[0], recv_sem=round_rcv.at[0], device_id=to_x, device_id_type=MESH)

    def send_rest():
        rest = pl.ds(ROUND_N, TN - ROUND_N)
        return pltpu.make_async_remote_copy(
            src_ref=p_snd.at[n_here - 1, tail_rows, rest], dst_ref=p_rcv.at[n_here - 1, tail_rows, rest],
            send_sem=round_snd.at[2], recv_sem=round_rcv.at[2], device_id=to_x, device_id_type=MESH)

    early = pl.ds(0, EARLY)

    def send_early():
        return pltpu.make_async_remote_copy(
            src_ref=nbr_ref.at[early], dst_ref=early_rcv, send_sem=early_sem.at[0], recv_sem=early_sem.at[1],
            device_id=to_x, device_id_type=MESH)

    def go_round(step):
        src = p_snd.at[n_here - 1, tail_rows, pl.ds(0, ROUND_N)] if step == 0 else round_buf
        dst = p_rcv.at[n_here - 1, tail_rows, pl.ds(0, ROUND_N)] if step == 2 else round_buf
        return pltpu.make_async_remote_copy(
            src_ref=src, dst_ref=dst, send_sem=round_snd.at[1], recv_sem=round_rcv.at[0 if step == 2 else 1],
            device_id=to_x if step == 1 else to_y, device_id_type=MESH)

    def send_c(j, h):
        return pltpu.make_async_remote_copy(
            src_ref=p_snd.at[j, pl.ds(h * half, half), :], dst_ref=p_rcv.at[j, pl.ds(h * half, half), :],
            send_sem=c_snd_sem.at[j, h], recv_sem=c_rcv_sem.at[j, h], device_id=to_x, device_id_type=MESH)

    barrier = pltpu.get_barrier_semaphore()
    for peer in (to_x, {"depth": 0, "col": lax.rem(col + 1 - depth, 2)}):
        pl.semaphore_signal(barrier, inc=1, device_id=peer, device_id_type=MESH)
    pl.semaphore_wait(barrier, 3 - 2 * depth)

    for i in range(4):
        send_a(i).start()

    @pl.when(depth == 0)
    def _():
        for i in range(4, last):
            send_a(i).start()
        for i in range(2):
            hand_over(i).start()
        pl.semaphore_signal(pair_sem, inc=1, device_id=to_y, device_id_type=MESH)
        pl.semaphore_wait(pair_sem, 1)
        pl.semaphore_signal(core_sem, inc=1, device_id=to_d, device_id_type=MESH)

    @pl.when(depth == 1)
    def _():
        pl.semaphore_wait(core_sem, 1)

    @pl.loop(0, n_chunks)
    def _(j):
        send_b(j).start()

    for place in range(4):
        load_a(place).start()

    def bring(j):
        send_d(j).start()
        load_b(j).start()

    for j in range(AHEAD):
        bring(j)

    @pl.when(depth == 1)
    def _():
        for i in range(2):
            hand_over(i).wait_recv()
            send_for_other(i).start()
        for i in range(4, last + 2):
            send_a(i).start()

    for place in range(4):
        load_a(place).wait()

    def part(j, h):
        p_snd[j, pl.ds(h * half, half), :] = jnp.dot(
            a_nbr[pl.ds(h * half, half), :], b_buf[j], preferred_element_type=jnp.float32)

    def gather(j):
        send_b(j).wait_recv()
        relay(j).start()

        @pl.when(j < n_chunks - AHEAD)
        def _():
            bring(j + AHEAD)

        load_b(j).wait()
        send_d(j).wait_recv()
        relay(j).wait_recv()

    @pl.loop(0, n_here)
    def _(j):
        gather(j)

        @pl.when(j == 0)
        def _():
            for i in range(4):
                send_a(i).wait_recv()

        @pl.when(j == LAG)
        def _():
            for i in range(4, last + 2):
                send_a(i).wait_recv()

        part(j, 0)

        @pl.when(j >= LAG)
        def _():
            part(j - LAG, 1)
            send_c(j, 0).start()

        p_own[j] = jnp.dot(a_own[...], b_buf[j], preferred_element_type=jnp.float32)

        @pl.when(j < LAG)
        def _():
            send_c(j, 0).start()

        @pl.when(j >= LAG)
        def _():
            send_c(j - LAG, 1).start()

    @pl.loop(n_here - LAG, n_here)
    def _(j):
        part(j, 1)

    def send_last():
        piece = pl.ds(half, half - ROUND)
        return pltpu.make_async_remote_copy(
            src_ref=p_snd.at[n_here - 1, piece, :], dst_ref=p_rcv.at[n_here - 1, piece, :],
            send_sem=c_snd_sem.at[n_here - 1, 1], recv_sem=c_rcv_sem.at[n_here - 1, 1],
            device_id=to_x, device_id_type=MESH)

    def add(j, piece):
        c_ref[piece, cols(j)] = (p_own[j, piece, :] + p_rcv[j, piece, :]).astype(c_ref.dtype)

    def finish(j):
        for h in range(2):
            send_c(j, h).wait_recv()
            add(j, pl.ds(h * half, half))

    finish(0)
    for j in range(n_here - LAG, n_here - 1):
        send_c(j, 1).start()

    @pl.when(source)
    def _():
        go_round(0).start()

    @pl.when(first_relay)
    def _():
        go_round(0).wait_recv()
        go_round(1).start()

    send_rest().start()
    send_last().start()

    @pl.when(jnp.logical_not(source))
    def _():
        send_tail().start()

    gather(n_chunks - 1)
    nbr_ref[...] = jnp.dot(a_nbr[...], b_buf[n_chunks - 1], preferred_element_type=jnp.float32)
    own_ref[...] = jnp.dot(a_own[...], b_buf[n_chunks - 1], preferred_element_type=jnp.float32)

    @pl.when(depth == 1)
    def _():
        send_early().start()

    @pl.loop(1, n_here - LAG)
    def _(j):
        finish(j)

    for i in range(last):
        send_a(i).wait_send()

    @pl.when(depth == 0)
    def _():
        for i in range(2):
            hand_over(i).wait_send()

    @pl.when(depth == 1)
    def _():
        for i in range(2):
            send_a(last + i).wait_send()
            send_for_other(i).wait_send()

    @pl.loop(0, n_chunks)
    def _(j):
        send_b(j).wait_send()
        send_d(j).wait_send()
        relay(j).wait_send()

    @pl.loop(0, n_here - LAG)
    def _(j):
        for h in range(2):
            send_c(j, h).wait_send()

    for j in range(n_here - LAG, n_here - 1):
        finish(j)
        for h in range(2):
            send_c(j, h).wait_send()

    @pl.when(second_relay)
    def _():
        go_round(1).wait_recv()
        go_round(2).start()

    send_c(n_here - 1, 0).wait_recv()
    add(n_here - 1, pl.ds(0, half))
    send_last().wait_recv()
    add(n_here - 1, pl.ds(half, half - ROUND))
    send_rest().wait_recv()
    send_tail().wait_recv()
    add(n_here - 1, tail_rows)

    @pl.when(source | first_relay | second_relay)
    def _():
        go_round(0).wait_send()

    @pl.when(depth == 1)
    def _():
        send_early().wait_recv()
        c_ref[early, cols(n_chunks - 1)] = (own_ref[early, :] + early_rcv[...]).astype(c_ref.dtype)
        send_early().wait_send()

    send_c(n_here - 1, 0).wait_send()
    send_last().wait_send()
    send_rest().wait_send()

    @pl.when(jnp.logical_not(source))
    def _():
        send_tail().wait_send()


def last_kernel(own_ref, nbr_ref, out_ref, c_ref, rcv, snd_sem, rcv_sem):
    to_x = {"row": 1 - lax.axis_index("row")}
    depth = lax.axis_index("depth")
    rows = own_ref.shape[0]
    pieces = [pl.ds(0, EARLY), pl.ds(EARLY, rows - EARLY)]

    def send(i):
        return pltpu.make_async_remote_copy(
            src_ref=nbr_ref.at[pieces[i]], dst_ref=rcv.at[pieces[i]], send_sem=snd_sem.at[i], recv_sem=rcv_sem.at[i],
            device_id=to_x, device_id_type=MESH)

    def add(i):
        c_ref[pieces[i], :] = (own_ref[pieces[i], :] + rcv[pieces[i], :]).astype(c_ref.dtype)

    barrier = pltpu.get_barrier_semaphore()
    pl.semaphore_signal(barrier, inc=1, device_id=to_x, device_id_type=MESH)
    pl.semaphore_wait(barrier, 1)

    @pl.when(depth == 0)
    def _():
        send(0).start()

    send(1).start()

    @pl.when(depth == 0)
    def _():
        send(0).wait_recv()
        add(0)

    send(1).wait_recv()
    add(1)

    @pl.when(depth == 0)
    def _():
        send(0).wait_send()

    send(1).wait_send()


def write_first(c_ref, out_ref, sem):
    depth = lax.axis_index("depth")
    n, tail = c_ref.shape[1] - TN, pl.ds(c_ref.shape[1] - TN, TN)
    early = pl.ds(0, EARLY)
    copy = pltpu.make_async_copy(c_ref.at[:, pl.ds(0, n)], out_ref.at[:, pl.ds(0, n)], sem.at[0])
    more = pltpu.make_async_copy(c_ref.at[early, tail], out_ref.at[early, tail], sem.at[1])
    copy.start()

    @pl.when(depth == 1)
    def _():
        more.start()
        more.wait()

    copy.wait()


def write_last(whole_ref, c_ref, out_ref, sem):
    depth = lax.axis_index("depth")
    tail = pl.ds(out_ref.shape[1] - TN, TN)
    early, late = pl.ds(0, EARLY), pl.ds(EARLY, c_ref.shape[0] - EARLY)
    copy = pltpu.make_async_copy(c_ref.at[late], out_ref.at[late, tail], sem.at[0])
    more = pltpu.make_async_copy(c_ref.at[early], out_ref.at[early, tail], sem.at[1])
    copy.start()

    @pl.when(depth == 0)
    def _():
        more.start()
        more.wait()

    copy.wait()


def solution(mesh):
    all_axes = ("depth", "row", "col")

    def device_block(a_rows, b_rows):
        rows, depth = a_rows.shape
        k_rows, n = b_rows.shape
        k = 4 * k_rows
        n_chunks = n // TN
        dma = pltpu.SemaphoreType.DMA
        n_here = n_chunks - 1
        f32 = jnp.float32
        vmem, any_space = pl.BlockSpec(memory_space=pltpu.VMEM), pl.BlockSpec(memory_space=pl.ANY)
        kept = 2 * rows * n + 8 * rows * TN
        regular = pltpu.SemaphoreType.REGULAR
        c, own, nbr = pl.pallas_call(
            kernel,
            out_shape=(pltpu.VMEM((rows, n), jnp.bfloat16),
                       pltpu.VMEM((rows, TN), f32), pltpu.VMEM((rows, TN), f32)),
            in_specs=[any_space] * 2,
            out_specs=(vmem,) * 3,
            scratch_shapes=[
                pltpu.VMEM((n_chunks, k, TN), jnp.bfloat16),
                pltpu.VMEM((rows, k), jnp.bfloat16),
                pltpu.VMEM((rows, k), jnp.bfloat16),
                pltpu.VMEM((n_here, rows, TN), f32),
                pltpu.VMEM((n_here, rows, TN), f32),
                pltpu.VMEM((n_here, rows, TN), f32),
                pltpu.VMEM((2, EXTRA, k_rows), jnp.bfloat16),
                dma((4,)), dma((n_chunks,)),
                dma((10,)), dma((10,)),
                dma((n_chunks,)), dma((n_chunks,)),
                dma((n_chunks,)), dma((n_chunks,)),
                dma((n_chunks,)), dma((n_chunks,)),
                dma((n_here, 2)), dma((n_here, 2)),
                dma((2,)), dma((2,)), dma((2,)),
                regular, regular,
                pltpu.VMEM((ROUND, ROUND_N), f32), dma((3,)), dma((3,)),
                pltpu.VMEM((EARLY, TN), f32), dma((2,)),
            ],
            compiler_params=pltpu.CompilerParams(
                collective_id=0, has_side_effects=True, vmem_limit_bytes=67043328 - kept),
        )(a_rows, b_rows)
        in_vmem = lambda x: pltpu.with_memory_space_constraint(x, pltpu.VMEM)
        small = pltpu.CompilerParams(vmem_limit_bytes=2 ** 20)
        whole = jax.ShapeDtypeStruct((rows, n), jnp.bfloat16)
        out = pl.pallas_call(
            write_first, out_shape=whole, in_specs=[vmem], out_specs=any_space,
            scratch_shapes=[dma((2,))], compiler_params=small)(in_vmem(c))
        c_last = pl.pallas_call(
            last_kernel,
            out_shape=pltpu.VMEM((rows, TN), jnp.bfloat16),
            in_specs=[vmem, vmem, pl.BlockSpec(memory_space=pltpu.HBM)],
            out_specs=vmem,
            scratch_shapes=[pltpu.VMEM((rows, TN), f32), dma((2,)), dma((2,))],
            compiler_params=pltpu.CompilerParams(
                collective_id=1, has_side_effects=True, vmem_limit_bytes=2 ** 23),
        )(in_vmem(own), in_vmem(nbr), pltpu.with_memory_space_constraint(out, pltpu.HBM))
        return pl.pallas_call(
            write_last, out_shape=whole, in_specs=[any_space, vmem], out_specs=any_space,
            scratch_shapes=[dma((2,))], input_output_aliases={0: 0}, compiler_params=small)(out, in_vmem(c_last))

    return jax.shard_map(device_block, mesh=mesh, in_specs=(P(all_axes, None), P(all_axes, None)),
                         out_specs=P(all_axes, None), check_vma=False)
```

profile of v0, /device:TPU:1, one launch (start us, length us, event | category | flops | bytes accessed | tf_op | source)
XLA Modules:
  0.0 222.5 jit_solution(10430417726613389100)
XLA Ops:
  0.0 214.7 %shard_map.28 = (bf16[384,5120]{1,0:T(8,128)(2,1)S(1)}, f32[384,512]{1,0:T(8,128)S(1)}, f32[384,512]{1,0:T(8,128)S(1)}) custom-call(bf16[384,6144]{1,0:T(8,128)(2,1)} %a_ref.1, bf16[768,5120]{1,0:T(8,128)(2,1)} %b_ref.1), custom_call_target="tpu_custom_call" | custom-call | tf_op jit(solution)/shard_map/pallas_call | solution.py:411
  214.7 1.9 shard_map.29.out_ref.whole_ref
  216.6 5.3 %shard_map.30.c_ref = bf16[384,512]{1,0:T(8,128)(2,1)S(1)} custom-call(f32[384,512]{1,0:T(8,128)S(1)} %get-tuple-element.9.own_ref, f32[384,512]{1,0:T(8,128)S(1)} %get-tuple-element.10.nbr_ref, bf16[384,5120]{1,0:T(8,128)(2,1)} %shard_map.29.out_ref.whole_ref), custom_call_target="tpu_custom_call" | custom-call | tf_op jit(solution)/shard_map/pallas_call | solution.py:445
  221.9 0.7 shard_map.31
where the time goes:
time: 223 us
  Pallas kernels  223 us (100%)
    pallas_call x1, Pallas kernels, device_block(): pl.pallas_call(kernel, out_shape=(pltpu.VMEM((rows, n), jnp.bfloat16), pl...  215 us
    pallas_call x1, Pallas kernels, device_block(): pl.pallas_call(last_kernel, out_shape=pltpu.VMEM((rows, TN), jnp.bfloat16...  5.26 us

commit v1 on v0

--- a/solution.py
+++ b/solution.py
@@ -82,9 +82,6 @@
             send_sem=r_snd_sem.at[j], recv_sem=r_rcv_sem.at[j], device_id=to_d, device_id_type=MESH)
 
     tail_rows = pl.ds(rows - ROUND, ROUND)
-    source = (depth == 1) & (row == 1) & (col == 0)
-    first_relay = (depth == 1) & (row == 1) & (col == 1)
-    second_relay = (depth == 1) & (row == 0) & (col == 1)
 
     def send_tail():
         return pltpu.make_async_remote_copy(
@@ -117,7 +114,7 @@
             send_sem=c_snd_sem.at[j, h], recv_sem=c_rcv_sem.at[j, h], device_id=to_x, device_id_type=MESH)
 
     barrier = pltpu.get_barrier_semaphore()
-    for peer in (to_x, {"depth": 0, "col": lax.rem(col + 1 - depth, 2)}):
+    for peer in (to_x, {"depth": 0, "col": (1 - depth - col) * (1 - depth - col)}):
         pl.semaphore_signal(barrier, inc=1, device_id=peer, device_id_type=MESH)
     pl.semaphore_wait(barrier, 3 - 2 * depth)
 
@@ -230,6 +227,9 @@
             add(j, pl.ds(h * half, half))
 
     finish(0)
+    source = (depth == 1) & (row == 1) & (col == 0)
+    first_relay = (depth == 1) & (row == 1) & (col == 1)
+    second_relay = (depth == 1) & (row == 0) & (col == 1)
     for j in range(n_here - LAG, n_here - 1):
         send_c(j, 1).start()
 
@@ -327,15 +327,17 @@
     to_x = {"row": 1 - lax.axis_index("row")}
     depth = lax.axis_index("depth")
     rows = own_ref.shape[0]
-    pieces = [pl.ds(0, EARLY), pl.ds(EARLY, rows - EARLY)]
-
-    def send(i):
-        return pltpu.make_async_remote_copy(
-            src_ref=nbr_ref.at[pieces[i]], dst_ref=rcv.at[pieces[i]], send_sem=snd_sem.at[i], recv_sem=rcv_sem.at[i],
+
+    def send(piece):
+        return pltpu.make_async_remote_copy(
+            src_ref=nbr_ref.at[piece], dst_ref=rcv.at[piece], send_sem=snd_sem, recv_sem=rcv_sem,
             device_id=to_x, device_id_type=MESH)
 
-    def add(i):
-        c_ref[pieces[i], :] = (own_ref[pieces[i], :] + rcv[pieces[i], :]).astype(c_ref.dtype)
+    def exchange(piece):
+        send(piece).start()
+        send(piece).wait_recv()
+        c_ref[piece, :] = (own_ref[piece, :] + rcv[piece, :]).astype(c_ref.dtype)
+        send(piece).wait_send()
 
     barrier = pltpu.get_barrier_semaphore()
     pl.semaphore_signal(barrier, inc=1, device_id=to_x, device_id_type=MESH)
@@ -343,23 +345,11 @@
 
     @pl.when(depth == 0)
     def _():
-        send(0).start()
-
-    send(1).start()
-
-    @pl.when(depth == 0)
-    def _():
-        send(0).wait_recv()
-        add(0)
-
-    send(1).wait_recv()
-    add(1)
-
-    @pl.when(depth == 0)
-    def _():
-        send(0).wait_send()
-
-    send(1).wait_send()
+        exchange(pl.ds(0, rows))
+
+    @pl.when(depth == 1)
+    def _():
+        exchange(pl.ds(EARLY, rows - EARLY))
 
 
 def write_first(c_ref, out_ref, sem):
@@ -381,17 +371,19 @@
 def write_last(whole_ref, c_ref, out_ref, sem):
     depth = lax.axis_index("depth")
     tail = pl.ds(out_ref.shape[1] - TN, TN)
-    early, late = pl.ds(0, EARLY), pl.ds(EARLY, c_ref.shape[0] - EARLY)
-    copy = pltpu.make_async_copy(c_ref.at[late], out_ref.at[late, tail], sem.at[0])
-    more = pltpu.make_async_copy(c_ref.at[early], out_ref.at[early, tail], sem.at[1])
-    copy.start()
+
+    def write(piece):
+        copy = pltpu.make_async_copy(c_ref.at[piece], out_ref.at[piece, tail], sem)
+        copy.start()
+        copy.wait()
 
     @pl.when(depth == 0)
     def _():
-        more.start()
-        more.wait()
-
-    copy.wait()
+        write(pl.ds(0, c_ref.shape[0]))
+
+    @pl.when(depth == 1)
+    def _():
+        write(pl.ds(EARLY, c_ref.shape[0] - EARLY))
 
 
 def solution(mesh):
@@ -447,13 +439,13 @@
             out_shape=pltpu.VMEM((rows, TN), jnp.bfloat16),
             in_specs=[vmem, vmem, pl.BlockSpec(memory_space=pltpu.HBM)],
             out_specs=vmem,
-            scratch_shapes=[pltpu.VMEM((rows, TN), f32), dma((2,)), dma((2,))],
+            scratch_shapes=[pltpu.VMEM((rows, TN), f32), dma, dma],
             compiler_params=pltpu.CompilerParams(
                 collective_id=1, has_side_effects=True, vmem_limit_bytes=2 ** 23),
         )(in_vmem(own), in_vmem(nbr), pltpu.with_memory_space_constraint(out, pltpu.HBM))
         return pl.pallas_call(
             write_last, out_shape=whole, in_specs=[any_space, vmem], out_specs=any_space,
-            scratch_shapes=[dma((2,))], input_output_aliases={0: 0}, compiler_params=small)(out, in_vmem(c_last))
+            scratch_shapes=[dma], input_output_aliases={0: 0}, compiler_params=small)(out, in_vmem(c_last))
 
     return jax.shard_map(device_block, mesh=mesh, in_specs=(P(all_axes, None), P(all_axes, None)),
                          out_specs=P(all_axes, None), check_vma=False)

time: 223 us -> 223 us (level)
  no operation moved by 1% of the time
where the time goes in v1:
time: 223 us
  Pallas kernels  222 us (100%)
    pallas_call x1, Pallas kernels, device_block(): pl.pallas_call(kernel, out_shape=(pltpu.VMEM((rows, n), jnp.bfloat16), pl...  215 us
    pallas_call x1, Pallas kernels, device_block(): pl.pallas_call(last_kernel, out_shape=pltpu.VMEM((rows, TN), jnp.bfloat16...  5.24 us

profile of v1, /device:TPU:1, one launch (start us, length us, event | category | flops | bytes accessed | tf_op | source)
XLA Modules:
  0.0 222.5 jit_solution(16957925949697563986)
XLA Ops:
  0.0 214.7 %shard_map.28 = (bf16[384,5120]{1,0:T(8,128)(2,1)S(1)}, f32[384,512]{1,0:T(8,128)S(1)}, f32[384,512]{1,0:T(8,128)S(1)}) custom-call(bf16[384,6144]{1,0:T(8,128)(2,1)} %a_ref.1, bf16[768,5120]{1,0:T(8,128)(2,1)} %b_ref.1), custom_call_target="tpu_custom_call" | custom-call | tf_op jit(solution)/shard_map/pallas_call | solution.py:403
  214.7 1.9 shard_map.29.out_ref.whole_ref
  216.6 5.2 %shard_map.30.c_ref = bf16[384,512]{1,0:T(8,128)(2,1)S(1)} custom-call(f32[384,512]{1,0:T(8,128)S(1)} %get-tuple-element.9.own_ref, f32[384,512]{1,0:T(8,128)S(1)} %get-tuple-element.10.nbr_ref, bf16[384,5120]{1,0:T(8,128)(2,1)} %shard_map.29.out_ref.whole_ref), custom_call_target="tpu_custom_call" | custom-call | tf_op jit(solution)/shard_map/pallas_call | solution.py:437
  221.9 0.7 shard_map.31

commit v2 on v1

--- a/solution.py
+++ b/solution.py
@@ -12,7 +12,7 @@
 ROUND = 16
 ROUND_N = 384
 EXTRA = 48
-EARLY = 304
+EARLY = 312
 
 
 def kernel(a_ref, b_ref, c_ref, own_ref, nbr_ref, b_buf, a_own, a_nbr, p_own, p_snd, p_rcv, a_fwd,
@@ -369,21 +369,24 @@
 
 
 def write_last(whole_ref, c_ref, out_ref, sem):
+    rows = c_ref.shape[0]
+    tail = pl.ds(out_ref.shape[1] - TN, TN)
+
+    def copy(start, size):
+        piece = pl.ds(start, size)
+        return pltpu.make_async_copy(c_ref.at[piece], out_ref.at[piece, tail], sem)
+
+    copy(EARLY, rows - EARLY).start()
     depth = lax.axis_index("depth")
-    tail = pl.ds(out_ref.shape[1] - TN, TN)
-
-    def write(piece):
-        copy = pltpu.make_async_copy(c_ref.at[piece], out_ref.at[piece, tail], sem)
-        copy.start()
-        copy.wait()
 
     @pl.when(depth == 0)
     def _():
-        write(pl.ds(0, c_ref.shape[0]))
-
-    @pl.when(depth == 1)
-    def _():
-        write(pl.ds(EARLY, c_ref.shape[0] - EARLY))
+        copy(0, EARLY).start()
+        copy(0, rows).wait()
+
+    @pl.when(depth == 1)
+    def _():
+        copy(EARLY, rows - EARLY).wait()
 
 
 def solution(mesh):

time: 223 us -> 223 us (level)
  no operation moved by 1% of the time
where the time goes in v2:
time: 223 us
  Pallas kernels  222 us (100%)
    pallas_call x1, Pallas kernels, device_block(): pl.pallas_call(kernel, out_shape=(pltpu.VMEM((rows, n), jnp.bfloat16), pl...  215 us
    pallas_call x1, Pallas kernels, device_block(): pl.pallas_call(last_kernel, out_shape=pltpu.VMEM((rows, TN), jnp.bfloat16...  4.89 us

profile of v2, /device:TPU:1, one launch (start us, length us, event | category | flops | bytes accessed | tf_op | source)
XLA Modules:
  0.0 222.5 jit_solution(1546813675624326119)
XLA Ops:
  0.0 215.0 %shard_map.28 = (bf16[384,5120]{1,0:T(8,128)(2,1)S(1)}, f32[384,512]{1,0:T(8,128)S(1)}, f32[384,512]{1,0:T(8,128)S(1)}) custom-call(bf16[384,6144]{1,0:T(8,128)(2,1)} %a_ref.1, bf16[768,5120]{1,0:T(8,128)(2,1)} %b_ref.1), custom_call_target="tpu_custom_call" | custom-call | tf_op jit(solution)/shard_map/pallas_call | solution.py:406
  215.0 1.9 shard_map.29.out_ref.whole_ref
  217.0 4.9 %shard_map.30.c_ref = bf16[384,512]{1,0:T(8,128)(2,1)S(1)} custom-call(f32[384,512]{1,0:T(8,128)S(1)} %get-tuple-element.9.own_ref, f32[384,512]{1,0:T(8,128)S(1)} %get-tuple-element.10.nbr_ref, bf16[384,5120]{1,0:T(8,128)(2,1)} %shard_map.29.out_ref.whole_ref), custom_call_target="tpu_custom_call" | custom-call | tf_op jit(solution)/shard_map/pallas_call | solution.py:440
  221.9 0.6 shard_map.31
